TPU v7x, 32 devices: a whole 2x2x4 slice. The times are simulated.
32 devices in a mesh: group: 2 (over x), tensor: 16 (over z, y, core).
Axes of the slice: x: 2, y: 2, z: 4, core: 2. Of those that a mesh axis runs over, the one named last changes fastest.
Arguments:
- z_star: bfloat16 [64, 5120], P(('group', 'tensor')), parts along dimension 0, may hold values from -6 to 6
- grad_out: float32 [64, 5120], P(('group', 'tensor')), parts along dimension 0, may hold values from -30 to 30
- w_gate: bfloat16 [10240, 13824], P('group', 'tensor'), parts along dimension 0, may hold values from -0.078125 to 0.078125
- w_up: bfloat16 [10240, 13824], P('group', 'tensor'), parts along dimension 0, may hold values from -0.078125 to 0.078125
- w_down: bfloat16 [27648, 5120], P(('group', 'tensor')), parts along dimension 0, may hold values from -0.0546875 to 0.0546875
- norm_gain: float32 [10240], P('group'), parts along dimension 0, may hold values from 0.5 to 1.5
- mix_rate: float32 [10240], P('group'), parts along dimension 0, may hold values from 0.3 to 1
Outputs:
- adjoint: float32 [64, 5120], P(('group', 'tensor')), parts along dimension 0
- grad_gate: bfloat16 [10240, 13824], P('group', 'tensor'), parts along dimension 0
- grad_up: bfloat16 [10240, 13824], P('group', 'tensor'), parts along dimension 0
- grad_down: bfloat16 [27648, 5120], P(('group', 'tensor')), parts along dimension 0
There are 2 independent parts, one for each index of `group`. A program takes and returns all parts, laid end to end along the dimension named above; each array names one. Nothing has to cross between parts.
All inputs are finite; a program needn't handle non-finite values.
Results may differ from a plain program's by a relative error of at most 0.014.
Values may be sent and summed in bfloat16 or wider, within the bound.
No kernel may reach another device: no remote copies, remote signals or barrier semaphores. Data moves between devices by JAX's collectives and lax.ppermute only.
A program may use at most 128 MiB of HBM per device.

v0:
```python
import jax
import jax.numpy as jnp
from jax import lax
from jax.sharding import PartitionSpec as P


def contract(left, right, left_dim, right_dim):
    return lax.dot_general(
        left, right, (((left_dim,), (right_dim,)), ((), ())), preferred_element_type=jnp.float32
    )


def normalize(z_rows, norm_gain):
    values = z_rows.astype(jnp.float32)
    root_mean = jnp.sqrt(jnp.mean(values * values, axis=-1, keepdims=True) + 1e-06)
    unit_rows = values / root_mean
    normed = (unit_rows * norm_gain).astype(jnp.bfloat16)
    return (root_mean, unit_rows, normed)


def norm_back(normed_grad, norm_gain, unit_rows, root_mean):
    scaled = norm_gain * normed_grad
    return (scaled - unit_rows * jnp.mean(scaled * unit_rows, axis=-1, keepdims=True)) / root_mean


def body(z_star, grad_out, w_gate, w_up, w_down, norm_gain, mix_rate):
    local_rows = z_star.shape[0]
    z_full = lax.all_gather(z_star, "tensor", axis=0, tiled=True)
    root_mean, unit_rows, normed = normalize(z_full, norm_gain)
    gate_pre = contract(normed, w_gate, 1, 0)
    lifted = contract(normed, w_up, 1, 0)
    sigma = jax.nn.sigmoid(gate_pre)
    gated = gate_pre * sigma
    slope = sigma * (1.0 + gate_pre * (1.0 - sigma))
    hidden = (gated * lifted).astype(jnp.bfloat16)

    def branch_rows(state_half):
        hidden_grad = contract(state_half, w_down, 1, 1)
        gate_grad = (hidden_grad * lifted * slope).astype(jnp.bfloat16)
        lift_grad = (hidden_grad * gated).astype(jnp.bfloat16)
        return (gate_grad, lift_grad)

    cotangent = lax.all_gather(grad_out.astype(jnp.bfloat16), "tensor", axis=0, tiled=True).astype(
        grad_out.dtype
    )

    def jacobian(state):
        gate_grad, lift_grad = branch_rows(state.astype(jnp.bfloat16))
        partial_sum = contract(gate_grad, w_gate, 1, 1) + contract(lift_grad, w_up, 1, 1)
        normed_grad = lax.psum(partial_sum, "tensor")
        return norm_back(normed_grad, norm_gain, unit_rows, root_mean)

    resid_zero = jacobian(cotangent)
    state_one = cotangent + mix_rate * resid_zero
    resid_one = cotangent + jacobian(state_one) - state_one
    resid_diff = resid_one - resid_zero
    blend = jnp.sum(resid_one * resid_diff) / (jnp.sum(resid_diff * resid_diff) + 1e-06)
    adjoint = (
        state_one - blend * (state_one - cotangent) + mix_rate * (resid_one - blend * resid_diff)
    )
    adjoint_half = adjoint.astype(jnp.bfloat16)
    gate_grad, lift_grad = branch_rows(adjoint_half)
    grad_gate = contract(normed, gate_grad, 0, 0)
    grad_up = contract(normed, lift_grad, 0, 0)
    grad_down = contract(hidden, adjoint_half, 0, 0)
    adjoint_own = lax.dynamic_slice_in_dim(
        adjoint, lax.axis_index("tensor") * local_rows, local_rows, 0
    )
    return (
        adjoint_own,
        grad_gate.astype(jnp.bfloat16),
        grad_up.astype(jnp.bfloat16),
        grad_down.astype(jnp.bfloat16),
    )


def solution(mesh):
    placed = (
        P(("group", "tensor"), None),
        P(("group", "tensor"), None),
        P("group", "tensor"),
        P("group", "tensor"),
        P(("group", "tensor"), None),
        P("group"),
        P("group"),
    )
    return jax.shard_map(
        body,
        mesh=mesh,
        in_specs=placed,
        out_specs=(
            P(("group", "tensor"), None),
            P("group", "tensor"),
            P("group", "tensor"),
            P(("group", "tensor"), None),
        ),
        check_vma=False,
    )
```

profile of v0, /device:TPU:0, one launch (start us, length us, event | category | flops | bytes accessed | tf_op | source)
XLA Modules:
  0.0 303.7 jit_solution(8700253727963858324)
XLA Ops:
  7.2 0.0 all-reduce.3.cloned.1.call-start
  7.2 0.8 convert_bitcast_fusion
  8.0 24.0 %all-gather = bf16[16,2,5120]{2,1,0:T(2,128)(2,1)S(1)} all-gather(bf16[1,2,5120]{2,1,0:T(2,128)(2,1)S(1)} %convert_bitcast_fusion), channel_id=1, replica_groups=mesh['group'=2,'tensor'=16] {'tensor'}, dimensions={0}, use_global_device_ids=true | all-gather | bytes 348160 | tf_op jit(solution)/shard_map/all_gather | solution.py:43
  32.0 0.1 reshape.27
  32.2 18.6 %all-gather.1 = bf16[16,2,5120]{2,1,0:T(2,128)(2,1)S(1)} all-gather(bf16[1,2,5120]{2,1,0:T(2,128)(2,1)} %bitcast.21), channel_id=1, replica_groups=mesh['group'=2,'tensor'=16] {'tensor'}, dimensions={0}, use_global_device_ids=true | all-gather | bytes 348160 | tf_op jit(solution)/shard_map/all_gather | solution.py:28
  50.7 0.1 reshape.30
  50.8 0.0 copy-start
  50.8 0.2 multiply_reduce_fusion.4
  51.0 1.0 multiply_convert_fusion
  52.0 0.0 copy-start.1
  52.1 6.6 %fusion.21 = f32[32,864]{1,0:T(8,128)S(1)} fusion(bf16[32,5120]{1,0:T(8,128)(2,1)S(1)} %multiply_convert_fusion, bf16[5120,864]{0,1:T(8,128)(2,1)} %param.9), kind=kOutput, calls=%fused_computation.45 | convolution fusion | flops 283115520 | bytes 9285632 | tf_op jit(solution)/shard_map/dot_general | solution.py:8
  58.7 0.0 copy-done
  58.7 0.0 slice-start
  58.7 0.0 slice-start.1
  58.8 2.7 fusion.20
  61.4 0.0 copy-done.1
  61.4 0.0 slice-start.2
  61.4 2.7 fusion.19
  64.1 0.0 slice-done
  64.1 0.0 slice-done.1
  64.1 0.0 slice-done.2
  64.2 1.6 fusion.12
  65.8 2.5 convolution_add_fusion.1
  68.3 0.0 all-reduce.3.cloned.1.call-update
  68.3 0.2 all-reduce.5.cloned.1.call-start
  68.5 90.0 %all-reduce.3.cloned.1.call-done = f32[32,5120]{1,0:T(8,128)} async-done(((f32[32,5120]{1,0:T(8,128)}), f32[32,5120]{1,0:T(8,128)}) %all-reduce.3.cloned.1.call-update) | async-done | bytes 655376 | tf_op jit(solution)/shard_map/psum | solution.py:50
  158.5 0.0 copy-done.2
  158.5 1.3 multiply_reduce_fusion.3
  159.8 1.3 subtract_divide_fusion
  161.1 0.0 copy-done.3
  161.1 0.0 slice-start.3
  161.1 0.0 slice-start.4
  161.1 6.3 %fusion.5 = f32[32,864]{1,0:T(8,128)S(1)} fusion(bf16[864,5120]{1,0:T(8,128)(2,1)} %param.11, f32[32,5120]{1,0:T(8,128)S(1)} %subtract_divide_fusion, bf16[32,5120]{1,0:T(8,128)(2,1)S(1)} %reshape.27, f32[5120]{0:T(1024)S(1)} %copy-done.3), kind=kOutput, calls=%fused_computation.20 | convolution fusion | flops 283770880 | bytes 9961472 | tf_op jit(solution)/shard_map/dot_general | solution.py:8
  167.5 0.0 slice-start.5
  167.5 5.3 %fusion.13 = f32[32,5120]{1,0:T(8,128)S(1)} fusion(bf16[5120,864]{0,1:T(8,128)(2,1)} %param.9, f32[32,864]{1,0:T(8,128)S(1)} %fusion.5, f32[32,864]{1,0:T(8,128)S(1)} %fusion.20, f32[32,864]{1,0:T(8,128)S(1)} %fusion.21), kind=kOutput, calls=%fused_computation.37 | convolution fusion | flops 283392000 | bytes 9834496 | tf_op jit(solution)/shard_map/dot_general | solution.py:8
  172.8 0.0 slice-done.3
  172.8 0.0 slice-done.4
  172.8 2.5 convolution_add_fusion
  175.3 0.0 all-reduce.5.cloned.1.call-update
  175.3 91.6 %all-reduce.5.cloned.1.call-done = f32[32,5120]{1,0:T(8,128)} async-done(((f32[32,5120]{1,0:T(8,128)}), f32[32,5120]{1,0:T(8,128)}) %all-reduce.5.cloned.1.call-update) | async-done | bytes 655376 | tf_op jit(solution)/shard_map/psum | solution.py:50
  266.9 1.3 multiply_reduce_fusion.2
  268.2 2.1 multiply_reduce_fusion
  271.6 0.2 fusion.3
  271.8 6.1 %fusion.9 = f32[32,864]{1,0:T(8,128)S(1)} fusion(bf16[864,5120]{1,0:T(8,128)(2,1)} %param.11, f32[32,5120]{1,0:T(8,128)S(1)} %fusion.3), kind=kOutput, calls=%fused_computation.24 | convolution fusion | flops 283279360 | bytes 9613312 | tf_op jit(solution)/shard_map/dot_general | solution.py:8
  278.0 6.1 %convolution_convert_fusion = bf16[864,5120]{1,0:T(8,128)(2,1)} fusion(f32[32,5120]{1,0:T(8,128)S(1)} %fusion.3, f32[32,864]{1,0:T(8,128)S(1)} %fusion.20, f32[32,864]{1,0:T(8,128)S(1)} %fusion.21), kind=kOutput, calls=%fused_computation | convolution fusion | flops 287868928 | bytes 9723904 | tf_op jit(solution)/shard_map/dot_general | solution.py:8
  284.1 6.1 %convolution_convert_fusion.2 = bf16[5120,864]{0,1:T(8,128)(2,1)} fusion(bf16[32,5120]{1,0:T(8,128)(2,1)S(1)} %multiply_convert_fusion, f32[32,864]{1,0:T(8,128)S(1)} %fusion.9, f32[32,864]{1,0:T(8,128)S(1)} %fusion.20, f32[32,864]{1,0:T(8,128)S(1)} %fusion.21), kind=kOutput, calls=%fused_computation.2 | convolution fusion | flops 287815680 | bytes 9506816 | tf_op jit(solution)/shard_map/dot_general | solution.py:8
  290.1 6.1 %convolution_convert_fusion.1 = bf16[5120,864]{0,1:T(8,128)(2,1)} fusion(bf16[32,5120]{1,0:T(8,128)(2,1)S(1)} %multiply_convert_fusion, f32[32,864]{1,0:T(8,128)S(1)} %fusion.9, f32[32,864]{1,0:T(8,128)S(1)} %fusion.21), kind=kOutput, calls=%fused_computation.1 | convolution fusion | flops 287705088 | bytes 9396224 | tf_op jit(solution)/shard_map/dot_general | solution.py:8
  296.2 0.6 constant_dynamic-slice_fusion
  (8 shorter events, 0.0 us)
Async XLA Ops:
  7.2 151.3 %all-reduce.3.cloned.1.call-start = ((), (), s32[]{:S(2)}) async-start(), calls=%async_computation | async-start | bytes 1310720 | tf_op jit(solution)/shard_map/psum | solution.py:50
  50.8 7.9 %copy-start = (bf16[5120,864]{0,1:T(8,128)(2,1)S(1)}, bf16[5120,864]{0,1:T(8,128)(2,1)}, u32[]{:S(2)}) copy-start(bf16[5120,864]{0,1:T(8,128)(2,1)} %param.10) | copy-start | bytes 26542084
  52.0 9.4 %copy-start.1 = (bf16[864,5120]{1,0:T(8,128)(2,1)S(1)}, bf16[864,5120]{1,0:T(8,128)(2,1)}, u32[]{:S(2)}) copy-start(bf16[864,5120]{1,0:T(8,128)(2,1)} %param.11) | copy-start | bytes 26542084
  58.7 5.4 %slice-start = ((s8[8847360]{0:T(1024)(128)(4,1)}), s8[4194304]{0:T(1024)(128)(4,1)S(1)}, s32[]{:S(2)}) async-start(s8[8847360]{0:T(1024)(128)(4,1)} %bitcast.17), calls=%async_computation.2 | async-start | bytes 8388608
  58.7 5.4 %slice-start.1 = ((s8[8847360]{0:T(1024)(128)(4,1)}), s8[4194304]{0:T(1024)(128)(4,1)S(1)}, s32[]{:S(2)}) async-start(s8[8847360]{0:T(1024)(128)(4,1)} %bitcast.17), calls=%async_computation.3 | async-start | bytes 8388608
  61.4 2.7 slice-start.2
  65.8 92.7 %copy-start.2 = (f32[5120]{0:T(1024)S(1)}, f32[5120]{0:T(1024)}, u32[]{:S(2)}) copy-start(f32[5120]{0:T(1024)} %param.12) | copy-start | bytes 61444
  65.8 95.3 %copy-start.3 = (f32[5120]{0:T(1024)S(1)}, f32[5120]{0:T(1024)}, u32[]{:S(2)}) copy-start(f32[5120]{0:T(1024)} %param.13) | copy-start | bytes 61444
  68.3 198.6 %all-reduce.5.cloned.1.call-start = ((), (), s32[]{:S(2)}) async-start(), calls=%async_computation.1 | async-start | bytes 1310720 | tf_op jit(solution)/shard_map/psum | solution.py:50
  161.1 11.6 %slice-start.3 = ((s8[8847360]{0:T(1024)(128)(4,1)}), s8[4194304]{0:T(1024)(128)(4,1)S(1)}, s32[]{:S(2)}) async-start(s8[8847360]{0:T(1024)(128)(4,1)} %bitcast.19), calls=%async_computation.5 | async-start | bytes 8388608
  161.1 11.6 %slice-start.4 = ((s8[8847360]{0:T(1024)(128)(4,1)}), s8[458752]{0:T(1024)(128)(4,1)S(1)}, s32[]{:S(2)}) async-start(s8[8847360]{0:T(1024)(128)(4,1)} %bitcast.19), calls=%async_computation.6 | async-start | bytes 917504
  167.5 5.3 %slice-start.5 = ((s8[8847360]{0:T(1024)(128)(4,1)}), s8[4194304]{0:T(1024)(128)(4,1)S(1)}, s32[]{:S(2)}) async-start(s8[8847360]{0:T(1024)(128)(4,1)} %bitcast.19), calls=%async_computation.7 | async-start | bytes 8388608
Sparse Core Ops, SparseCore 0:
  68.4 90.0 all-reduce.2
  175.4 91.4 all-reduce.4
where the time goes:
time: 304 us
  waiting for transfers between devices  182 us (60%)
  matrix products  54.4 us (18%)
  blocking collectives  42.6 us (14%)
  between operations  15.5 us (5%)
  other arithmetic  8.24 us (3%)
    psum x2, waiting for transfers between devices, jacobian(): normed_grad = lax.psum(partial_sum, 'tensor')  182 us
    dot_general x12, matrix products, contract(): lax.dot_general(left, right, (((left_dim,), (right_dim,)), ((), ())), pre...  54.4 us
    all_gather x1, blocking collectives, body(): lax.all_gather(grad_out.astype(jnp.bfloat16), 'tensor', axis=0, tiled=True)  24 us
    all_gather x1, blocking collectives, body(): z_full = lax.all_gather(z_star, 'tensor', axis=0, tiled=True)  18.6 us
  transfers between devices with their start and end apart: 2, of which 2 were waited for; matrix products, arithmetic and copies ran while one was open for 0% of the time, Pallas kernels for 0%

commit v1 on v0

--- a/solution.py
+++ b/solution.py
@@ -25,7 +25,16 @@
 
 def body(z_star, grad_out, w_gate, w_up, w_down, norm_gain, mix_rate):
     local_rows = z_star.shape[0]
-    z_full = lax.all_gather(z_star, "tensor", axis=0, tiled=True)
+    count, index, rows = (lax.axis_size("tensor"), lax.axis_index("tensor"), z_star.shape[0])
+    forward = [(i, (i + 1) % count) for i in range(count)]
+    filled = jnp.zeros((*z_star.shape[:0], count * rows, *z_star.shape[0 + 1 :]), z_star.dtype)
+    current = z_star
+    for hop in range(count):
+        owner = (index - hop) % count
+        filled = lax.dynamic_update_slice_in_dim(filled, current, owner * rows, axis=0)
+        if hop < count - 1:
+            current = lax.ppermute(current, "tensor", forward)
+    z_full = filled
     root_mean, unit_rows, normed = normalize(z_full, norm_gain)
     gate_pre = contract(normed, w_gate, 1, 0)
     lifted = contract(normed, w_up, 1, 0)

time: 304 us -> 369 us (1.21)
  waiting for transfers between devices: 182 us -> 262 us
  blocking collectives: 42.6 us -> 23.6 us
    ppermute x0 -> x15, waiting for transfers between devices: none -> 81.8 us  [body(): current = lax.ppermute(current, 'tensor', forward)]
    all_gather x1 -> x0, blocking collectives: 18.6 us -> none  [body(): z_full = lax.all_gather(z_star, 'tensor', axis=0, tiled=True)]
  transfers between devices with their start and end apart: 2 -> 17, of which waited for: 2 -> 16; matrix products, arithmetic and copies ran while one was open for 0% -> 2% of each run, Pallas kernels for 0% -> 0%
where the time goes in v1:
time: 369 us
  waiting for transfers between devices  262 us (71%)
  matrix products  57.9 us (16%)
  blocking collectives  23.6 us (6%)
  between operations  16 us (4%)
  other arithmetic  6.31 us (2%)
    psum x2, waiting for transfers between devices, jacobian(): normed_grad = lax.psum(partial_sum, 'tensor')  181 us
    ppermute x15, waiting for transfers between devices, body(): current = lax.ppermute(current, 'tensor', forward)  81.8 us
    dot_general x12, matrix products, contract(): lax.dot_general(left, right, (((left_dim,), (right_dim,)), ((), ())), pre...  57.9 us
    all_gather x1, blocking collectives, body(): lax.all_gather(grad_out.astype(jnp.bfloat16), 'tensor', axis=0, tiled=True)  23.6 us
  transfers between devices with their start and end apart: 17, of which 16 were waited for; matrix products, arithmetic and copies ran while one was open for 2% of the time, Pallas kernels for 0%

profile of v1, /device:TPU:0, one launch (start us, length us, event | category | flops | bytes accessed | tf_op | source)
XLA Modules:
  0.0 368.7 jit_solution(9670303433625978515)
XLA Ops:
  7.2 0.0 all-reduce.3.cloned.1.call-start
  7.2 0.5 collective-permute-start
  7.8 0.8 convert_bitcast_fusion
  8.6 23.6 %all-gather = bf16[16,2,5120]{2,1,0:T(2,128)(2,1)S(1)} all-gather(bf16[1,2,5120]{2,1,0:T(2,128)(2,1)S(1)} %convert_bitcast_fusion), channel_id=1, replica_groups=mesh['group'=2,'tensor'=16] {'tensor'}, dimensions={0}, use_global_device_ids=true | all-gather | bytes 348160 | tf_op jit(solution)/shard_map/all_gather | solution.py:52
  32.1 0.1 reshape.27
  32.3 6.1 %fusion.24 = f32[32,864]{1,0:T(8,128)S(1)} fusion(bf16[32,5120]{1,0:T(8,128)(2,1)S(1)} %reshape.27, bf16[864,5120]{1,0:T(8,128)(2,1)} %param.11), kind=kOutput, calls=%fused_computation.63 | convolution fusion | flops 283115520 | bytes 9285632 | tf_op jit(solution)/shard_map/dot_general | solution.py:8
  38.4 0.1 broadcast_in_dim.2
  38.9 0.4 collective-permute-start.1
  39.3 5.5 %collective-permute-done.1 = bf16[2,5120]{1,0:T(2,128)(2,1)S(1)} collective-permute-done((bf16[2,5120]{1,0:T(2,128)(2,1)S(1)}, bf16[2,5120]{1,0:T(2,128)(2,1)S(1)}, u32[]{:S(2)}, u32[]{:S(2)}) %collective-permute-start.1) | collective-permute-done | bytes 20512 | tf_op jit(solution)/shard_map/ppermute | solution.py:36
  44.9 5.9 %collective-permute-done.2 = bf16[2,5120]{1,0:T(2,128)(2,1)S(1)} collective-permute-done((bf16[2,5120]{1,0:T(2,128)(2,1)S(1)}, bf16[2,5120]{1,0:T(2,128)(2,1)S(1)}, u32[]{:S(2)}, u32[]{:S(2)}) %collective-permute-start.2) | collective-permute-done | bytes 20512 | tf_op jit(solution)/shard_map/ppermute | solution.py:36
  50.8 5.9 %collective-permute-done.3 = bf16[2,5120]{1,0:T(2,128)(2,1)S(1)} collective-permute-done((bf16[2,5120]{1,0:T(2,128)(2,1)S(1)}, bf16[2,5120]{1,0:T(2,128)(2,1)S(1)}, u32[]{:S(2)}, u32[]{:S(2)}) %collective-permute-start.3) | collective-permute-done | bytes 20512 | tf_op jit(solution)/shard_map/ppermute | solution.py:36
  56.7 5.9 %collective-permute-done.4 = bf16[2,5120]{1,0:T(2,128)(2,1)S(1)} collective-permute-done((bf16[2,5120]{1,0:T(2,128)(2,1)S(1)}, bf16[2,5120]{1,0:T(2,128)(2,1)S(1)}, u32[]{:S(2)}, u32[]{:S(2)}) %collective-permute-start.4) | collective-permute-done | bytes 20512 | tf_op jit(solution)/shard_map/ppermute | solution.py:36
  62.6 5.9 %collective-permute-done.5 = bf16[2,5120]{1,0:T(2,128)(2,1)S(1)} collective-permute-done((bf16[2,5120]{1,0:T(2,128)(2,1)S(1)}, bf16[2,5120]{1,0:T(2,128)(2,1)S(1)}, u32[]{:S(2)}, u32[]{:S(2)}) %collective-permute-start.5) | collective-permute-done | bytes 20512 | tf_op jit(solution)/shard_map/ppermute | solution.py:36
  68.5 5.9 %collective-permute-done.6 = bf16[2,5120]{1,0:T(2,128)(2,1)S(1)} collective-permute-done((bf16[2,5120]{1,0:T(2,128)(2,1)S(1)}, bf16[2,5120]{1,0:T(2,128)(2,1)S(1)}, u32[]{:S(2)}, u32[]{:S(2)}) %collective-permute-start.6) | collective-permute-done | bytes 20512 | tf_op jit(solution)/shard_map/ppermute | solution.py:36
  74.4 5.9 %collective-permute-done.7 = bf16[2,5120]{1,0:T(2,128)(2,1)S(1)} collective-permute-done((bf16[2,5120]{1,0:T(2,128)(2,1)S(1)}, bf16[2,5120]{1,0:T(2,128)(2,1)S(1)}, u32[]{:S(2)}, u32[]{:S(2)}) %collective-permute-start.7) | collective-permute-done | bytes 20512 | tf_op jit(solution)/shard_map/ppermute | solution.py:36
  80.3 5.9 %collective-permute-done.8 = bf16[2,5120]{1,0:T(2,128)(2,1)S(1)} collective-permute-done((bf16[2,5120]{1,0:T(2,128)(2,1)S(1)}, bf16[2,5120]{1,0:T(2,128)(2,1)S(1)}, u32[]{:S(2)}, u32[]{:S(2)}) %collective-permute-start.8) | collective-permute-done | bytes 20512 | tf_op jit(solution)/shard_map/ppermute | solution.py:36
  86.2 5.9 %collective-permute-done.9 = bf16[2,5120]{1,0:T(2,128)(2,1)S(1)} collective-permute-done((bf16[2,5120]{1,0:T(2,128)(2,1)S(1)}, bf16[2,5120]{1,0:T(2,128)(2,1)S(1)}, u32[]{:S(2)}, u32[]{:S(2)}) %collective-permute-start.9) | collective-permute-done | bytes 20512 | tf_op jit(solution)/shard_map/ppermute | solution.py:36
  92.1 5.9 %collective-permute-done.10 = bf16[2,5120]{1,0:T(2,128)(2,1)S(1)} collective-permute-done((bf16[2,5120]{1,0:T(2,128)(2,1)S(1)}, bf16[2,5120]{1,0:T(2,128)(2,1)S(1)}, u32[]{:S(2)}, u32[]{:S(2)}) %collective-permute-start.10) | collective-permute-done | bytes 20512 | tf_op jit(solution)/shard_map/ppermute | solution.py:36
  98.0 5.9 %collective-permute-done.11 = bf16[2,5120]{1,0:T(2,128)(2,1)S(1)} collective-permute-done((bf16[2,5120]{1,0:T(2,128)(2,1)S(1)}, bf16[2,5120]{1,0:T(2,128)(2,1)S(1)}, u32[]{:S(2)}, u32[]{:S(2)}) %collective-permute-start.11) | collective-permute-done | bytes 20512 | tf_op jit(solution)/shard_map/ppermute | solution.py:36
  103.9 5.9 %collective-permute-done.12 = bf16[2,5120]{1,0:T(2,128)(2,1)S(1)} collective-permute-done((bf16[2,5120]{1,0:T(2,128)(2,1)S(1)}, bf16[2,5120]{1,0:T(2,128)(2,1)S(1)}, u32[]{:S(2)}, u32[]{:S(2)}) %collective-permute-start.12) | collective-permute-done | bytes 20512 | tf_op jit(solution)/shard_map/ppermute | solution.py:36
  109.8 5.9 %collective-permute-done.13 = bf16[2,5120]{1,0:T(2,128)(2,1)S(1)} collective-permute-done((bf16[2,5120]{1,0:T(2,128)(2,1)S(1)}, bf16[2,5120]{1,0:T(2,128)(2,1)S(1)}, u32[]{:S(2)}, u32[]{:S(2)}) %collective-permute-start.13) | collective-permute-done | bytes 20512 | tf_op jit(solution)/shard_map/ppermute | solution.py:36
  115.7 5.9 %collective-permute-done.14 = bf16[2,5120]{1,0:T(2,128)(2,1)S(1)} collective-permute-done((bf16[2,5120]{1,0:T(2,128)(2,1)S(1)}, bf16[2,5120]{1,0:T(2,128)(2,1)S(1)}, u32[]{:S(2)}, u32[]{:S(2)}) %collective-permute-start.14) | collective-permute-done | bytes 20512 | tf_op jit(solution)/shard_map/ppermute | solution.py:36
  121.6 0.2 fusion
  121.9 6.3 %fusion.19 = f32[32,864]{1,0:T(8,128)S(1)} fusion(bf16[5120,864]{0,1:T(8,128)(2,1)} %param.9, f32[5120]{0:T(1024)S(1)} %copy-done.2, f32[32]{0:T(128)S(1)} %add_sqrt_fusion, bf16[32,5120]{1,0:T(8,128)(2,1)S(1)} %constant_dynamic-update-slice_fusion), kind=kOutput, calls=%fused_computation.60 | convolution fusion | flops 283770880 | bytes 9306240 | tf_op jit(solution)/shard_map/dot_general | solution.py:8
  128.2 0.0 slice-start.2
  128.2 2.7 fusion.20
  131.0 1.6 fusion.13
  132.6 2.5 convolution_add_fusion.1
  135.1 0.0 all-reduce.3.cloned.1.call-update
  135.1 0.2 all-reduce.5.cloned.1.call-start
  135.3 88.9 %all-reduce.3.cloned.1.call-done = f32[32,5120]{1,0:T(8,128)} async-done(((f32[32,5120]{1,0:T(8,128)}), f32[32,5120]{1,0:T(8,128)}) %all-reduce.3.cloned.1.call-update) | async-done | bytes 655376 | tf_op jit(solution)/shard_map/psum | solution.py:59
  224.3 1.4 multiply_reduce_fusion.3
  225.6 0.0 slice-start.3
  225.6 6.5 %fusion.6 = f32[32,864]{1,0:T(8,128)S(1)} fusion(bf16[864,5120]{1,0:T(8,128)(2,1)} %param.11, bf16[32,5120]{1,0:T(8,128)(2,1)S(1)} %reshape.27, f32[5120]{0:T(1024)S(1)} %copy-done.3, f32[32,5120]{1,0:T(8,128)} %all-reduce.3.cloned.1.call-done, f32[32]{0:T(128)S(1)} %broadcast_multiply_fusion.1, f32[32]{0:T(128)S(1)} %add_sqrt_fusion, ...), kind=kOutput, calls=%fused_computation.22 | convolution fusion | flops 284753920 | bytes 10309888 | tf_op jit(solution)/shard_map/dot_general | solution.py:8
  232.2 0.0 slice-start.5
  232.2 5.3 %fusion.14 = f32[32,5120]{1,0:T(8,128)S(1)} fusion(bf16[5120,864]{0,1:T(8,128)(2,1)} %param.9, f32[32,864]{1,0:T(8,128)S(1)} %fusion.6, f32[32,864]{1,0:T(8,128)S(1)} %fusion.20, f32[32,864]{1,0:T(8,128)S(1)} %fusion.19), kind=kOutput, calls=%fused_computation.38 | convolution fusion | flops 283392000 | bytes 9834496 | tf_op jit(solution)/shard_map/dot_general | solution.py:8
  237.5 0.0 slice-done.4
  237.5 2.4 convolution_add_fusion
  240.0 0.0 all-reduce.5.cloned.1.call-update
  240.0 91.6 %all-reduce.5.cloned.1.call-done = f32[32,5120]{1,0:T(8,128)} async-done(((f32[32,5120]{1,0:T(8,128)}), f32[32,5120]{1,0:T(8,128)}) %all-reduce.5.cloned.1.call-update) | async-done | bytes 655376 | tf_op jit(solution)/shard_map/psum | solution.py:59
  331.6 1.4 multiply_reduce_fusion.2
  333.0 2.2 multiply_reduce_fusion
  336.5 0.4 fusion.4
  336.9 6.2 %fusion.10 = f32[32,864]{1,0:T(8,128)S(1)} fusion(bf16[864,5120]{1,0:T(8,128)(2,1)} %param.11, f32[32,5120]{1,0:T(8,128)S(1)} %fusion.4), kind=kOutput, calls=%fused_computation.25 | convolution fusion | flops 283279360 | bytes 9613312 | tf_op jit(solution)/shard_map/dot_general | solution.py:8
  343.0 6.1 %convolution_convert_fusion = bf16[864,5120]{1,0:T(8,128)(2,1)} fusion(f32[32,5120]{1,0:T(8,128)S(1)} %fusion.4, f32[32,864]{1,0:T(8,128)S(1)} %fusion.20, f32[32,864]{1,0:T(8,128)S(1)} %fusion.19), kind=kOutput, calls=%fused_computation | convolution fusion | flops 287868928 | bytes 9723904 | tf_op jit(solution)/shard_map/dot_general | solution.py:8
  349.1 6.1 %convolution_convert_fusion.2 = bf16[5120,864]{0,1:T(8,128)(2,1)} fusion(f32[32,864]{1,0:T(8,128)S(1)} %fusion.10, f32[32,864]{1,0:T(8,128)S(1)} %fusion.20, f32[32,864]{1,0:T(8,128)S(1)} %fusion.19, f32[5120]{0:T(1024)S(1)} %copy-done.2, f32[32]{0:T(128)S(1)} %add_sqrt_fusion, bf16[32,5120]{1,0:T(8,128)(2,1)S(1)} %constant_dynamic-update-slice_fusion), kind=kOutput, calls=%fused_computation.2 | convolution fusion | flops 288471040 | bytes 9527424 | tf_op jit(solution)/shard_map/dot_general | solution.py:8
  355.2 6.1 %convolution_convert_fusion.1 = bf16[5120,864]{0,1:T(8,128)(2,1)} fusion(f32[32,864]{1,0:T(8,128)S(1)} %fusion.10, f32[32,864]{1,0:T(8,128)S(1)} %fusion.19, f32[5120]{0:T(1024)S(1)} %copy-done.2, f32[32]{0:T(128)S(1)} %add_sqrt_fusion, bf16[32,5120]{1,0:T(8,128)(2,1)S(1)} %constant_dynamic-update-slice_fusion), kind=kOutput, calls=%fused_computation.1 | convolution fusion | flops 288360448 | bytes 9416832 | tf_op jit(solution)/shard_map/dot_general | solution.py:8
  361.3 0.6 constant_dynamic-slice_fusion
  (53 shorter events, 0.6 us)
Async XLA Ops:
  7.2 31.3 %copy-start.4 = (bf16[2,5120]{1,0:T(2,128)(2,1)S(1)}, bf16[2,5120]{1,0:T(2,128)(2,1)}, u32[]{:S(2)}) copy-start(bf16[2,5120]{1,0:T(2,128)(2,1)} %param.7) | copy-start | bytes 61444
  7.2 114.7 %copy-start.2 = (f32[5120]{0:T(1024)S(1)}, f32[5120]{0:T(1024)}, u32[]{:S(2)}) copy-start(f32[5120]{0:T(1024)} %param.12) | copy-start | bytes 61444
  7.2 217.1 %all-reduce.3.cloned.1.call-start = ((), (), s32[]{:S(2)}) async-start(), calls=%async_computation | async-start | bytes 1310720 | tf_op jit(solution)/shard_map/psum | solution.py:59
  7.2 31.6 %collective-permute-start = (bf16[2,5120]{1,0:T(2,128)(2,1)}, bf16[2,5120]{1,0:T(2,128)(2,1)S(1)}, u32[]{:S(2)}, u32[]{:S(2)}) collective-permute-start(bf16[2,5120]{1,0:T(2,128)(2,1)} %param.7), channel_id=1, source_target_pairs={{0,1},{1,2},{2,3},{3,4},{4,5},{5,6},{6,7},{7,8},{8,9},{9,10},{10,1... | collective-permute-start | bytes 61448 | tf_op jit(solution)/shard_map/ppermute | solution.py:36
  38.9 89.3 %copy-start = (bf16[5120,864]{0,1:T(8,128)(2,1)S(1)}, bf16[5120,864]{0,1:T(8,128)(2,1)}, u32[]{:S(2)}) copy-start(bf16[5120,864]{0,1:T(8,128)(2,1)} %param.10) | copy-start | bytes 26542084
  38.9 6.0 %collective-permute-start.1 = (bf16[2,5120]{1,0:T(2,128)(2,1)S(1)}, bf16[2,5120]{1,0:T(2,128)(2,1)S(1)}, u32[]{:S(2)}, u32[]{:S(2)}) collective-permute-start(bf16[2,5120]{1,0:T(2,128)(2,1)S(1)} %collective-permute-done), channel_id=1, source_target_pairs={{0,1},{1,2},{2,3},{3,4},{4,5},{5,6},{6,7},{7,8},{8,9},{9,10},{10,1... | collective-permute-start | bytes 61448 | tf_op jit(solution)/shard_map/ppermute | solution.py:36
  44.8 5.9 %collective-permute-start.2 = (bf16[2,5120]{1,0:T(2,128)(2,1)S(1)}, bf16[2,5120]{1,0:T(2,128)(2,1)S(1)}, u32[]{:S(2)}, u32[]{:S(2)}) collective-permute-start(bf16[2,5120]{1,0:T(2,128)(2,1)S(1)} %collective-permute-done.1), channel_id=1, source_target_pairs={{0,1},{1,2},{2,3},{3,4},{4,5},{5,6},{6,7},{7,8},{8,9},{9,10},{10,1... | collective-permute-start | bytes 61448 | tf_op jit(solution)/shard_map/ppermute | solution.py:36
  50.7 5.9 %collective-permute-start.3 = (bf16[2,5120]{1,0:T(2,128)(2,1)S(1)}, bf16[2,5120]{1,0:T(2,128)(2,1)S(1)}, u32[]{:S(2)}, u32[]{:S(2)}) collective-permute-start(bf16[2,5120]{1,0:T(2,128)(2,1)S(1)} %collective-permute-done.2), channel_id=1, source_target_pairs={{0,1},{1,2},{2,3},{3,4},{4,5},{5,6},{6,7},{7,8},{8,9},{9,10},{10,1... | collective-permute-start | bytes 61448 | tf_op jit(solution)/shard_map/ppermute | solution.py:36
  56.6 5.9 %collective-permute-start.4 = (bf16[2,5120]{1,0:T(2,128)(2,1)S(1)}, bf16[2,5120]{1,0:T(2,128)(2,1)S(1)}, u32[]{:S(2)}, u32[]{:S(2)}) collective-permute-start(bf16[2,5120]{1,0:T(2,128)(2,1)S(1)} %collective-permute-done.3), channel_id=1, source_target_pairs={{0,1},{1,2},{2,3},{3,4},{4,5},{5,6},{6,7},{7,8},{8,9},{9,10},{10,1... | collective-permute-start | bytes 61448 | tf_op jit(solution)/shard_map/ppermute | solution.py:36
  62.5 5.9 %collective-permute-start.5 = (bf16[2,5120]{1,0:T(2,128)(2,1)S(1)}, bf16[2,5120]{1,0:T(2,128)(2,1)S(1)}, u32[]{:S(2)}, u32[]{:S(2)}) collective-permute-start(bf16[2,5120]{1,0:T(2,128)(2,1)S(1)} %collective-permute-done.4), channel_id=1, source_target_pairs={{0,1},{1,2},{2,3},{3,4},{4,5},{5,6},{6,7},{7,8},{8,9},{9,10},{10,1... | collective-permute-start | bytes 61448 | tf_op jit(solution)/shard_map/ppermute | solution.py:36
  68.5 5.9 %collective-permute-start.6 = (bf16[2,5120]{1,0:T(2,128)(2,1)S(1)}, bf16[2,5120]{1,0:T(2,128)(2,1)S(1)}, u32[]{:S(2)}, u32[]{:S(2)}) collective-permute-start(bf16[2,5120]{1,0:T(2,128)(2,1)S(1)} %collective-permute-done.5), channel_id=1, source_target_pairs={{0,1},{1,2},{2,3},{3,4},{4,5},{5,6},{6,7},{7,8},{8,9},{9,10},{10,1... | collective-permute-start | bytes 61448 | tf_op jit(solution)/shard_map/ppermute | solution.py:36
  74.4 5.9 %collective-permute-start.7 = (bf16[2,5120]{1,0:T(2,128)(2,1)S(1)}, bf16[2,5120]{1,0:T(2,128)(2,1)S(1)}, u32[]{:S(2)}, u32[]{:S(2)}) collective-permute-start(bf16[2,5120]{1,0:T(2,128)(2,1)S(1)} %collective-permute-done.6), channel_id=1, source_target_pairs={{0,1},{1,2},{2,3},{3,4},{4,5},{5,6},{6,7},{7,8},{8,9},{9,10},{10,1... | collective-permute-start | bytes 61448 | tf_op jit(solution)/shard_map/ppermute | solution.py:36
  80.3 5.9 %collective-permute-start.8 = (bf16[2,5120]{1,0:T(2,128)(2,1)S(1)}, bf16[2,5120]{1,0:T(2,128)(2,1)S(1)}, u32[]{:S(2)}, u32[]{:S(2)}) collective-permute-start(bf16[2,5120]{1,0:T(2,128)(2,1)S(1)} %collective-permute-done.7), channel_id=1, source_target_pairs={{0,1},{1,2},{2,3},{3,4},{4,5},{5,6},{6,7},{7,8},{8,9},{9,10},{10,1... | collective-permute-start | bytes 61448 | tf_op jit(solution)/shard_map/ppermute | solution.py:36
  86.2 5.9 %collective-permute-start.9 = (bf16[2,5120]{1,0:T(2,128)(2,1)S(1)}, bf16[2,5120]{1,0:T(2,128)(2,1)S(1)}, u32[]{:S(2)}, u32[]{:S(2)}) collective-permute-start(bf16[2,5120]{1,0:T(2,128)(2,1)S(1)} %collective-permute-done.8), channel_id=1, source_target_pairs={{0,1},{1,2},{2,3},{3,4},{4,5},{5,6},{6,7},{7,8},{8,9},{9,10},{10,1... | collective-permute-start | bytes 61448 | tf_op jit(solution)/shard_map/ppermute | solution.py:36
  92.1 5.9 %collective-permute-start.10 = (bf16[2,5120]{1,0:T(2,128)(2,1)S(1)}, bf16[2,5120]{1,0:T(2,128)(2,1)S(1)}, u32[]{:S(2)}, u32[]{:S(2)}) collective-permute-start(bf16[2,5120]{1,0:T(2,128)(2,1)S(1)} %collective-permute-done.9), channel_id=1, source_target_pairs={{0,1},{1,2},{2,3},{3,4},{4,5},{5,6},{6,7},{7,8},{8,9},{9,10},{10,1... | collective-permute-start | bytes 61448 | tf_op jit(solution)/shard_map/ppermute | solution.py:36
  98.0 5.9 %collective-permute-start.11 = (bf16[2,5120]{1,0:T(2,128)(2,1)S(1)}, bf16[2,5120]{1,0:T(2,128)(2,1)S(1)}, u32[]{:S(2)}, u32[]{:S(2)}) collective-permute-start(bf16[2,5120]{1,0:T(2,128)(2,1)S(1)} %collective-permute-done.10), channel_id=1, source_target_pairs={{0,1},{1,2},{2,3},{3,4},{4,5},{5,6},{6,7},{7,8},{8,9},{9,10},{10,1... | collective-permute-start | bytes 61448 | tf_op jit(solution)/shard_map/ppermute | solution.py:36
  103.9 5.9 %collective-permute-start.12 = (bf16[2,5120]{1,0:T(2,128)(2,1)S(1)}, bf16[2,5120]{1,0:T(2,128)(2,1)S(1)}, u32[]{:S(2)}, u32[]{:S(2)}) collective-permute-start(bf16[2,5120]{1,0:T(2,128)(2,1)S(1)} %collective-permute-done.11), channel_id=1, source_target_pairs={{0,1},{1,2},{2,3},{3,4},{4,5},{5,6},{6,7},{7,8},{8,9},{9,10},{10,1... | collective-permute-start | bytes 61448 | tf_op jit(solution)/shard_map/ppermute | solution.py:36
  109.8 5.9 %collective-permute-start.13 = (bf16[2,5120]{1,0:T(2,128)(2,1)S(1)}, bf16[2,5120]{1,0:T(2,128)(2,1)S(1)}, u32[]{:S(2)}, u32[]{:S(2)}) collective-permute-start(bf16[2,5120]{1,0:T(2,128)(2,1)S(1)} %collective-permute-done.12), channel_id=1, source_target_pairs={{0,1},{1,2},{2,3},{3,4},{4,5},{5,6},{6,7},{7,8},{8,9},{9,10},{10,1... | collective-permute-start | bytes 61448 | tf_op jit(solution)/shard_map/ppermute | solution.py:36
  115.7 5.9 %collective-permute-start.14 = (bf16[2,5120]{1,0:T(2,128)(2,1)S(1)}, bf16[2,5120]{1,0:T(2,128)(2,1)S(1)}, u32[]{:S(2)}, u32[]{:S(2)}) collective-permute-start(bf16[2,5120]{1,0:T(2,128)(2,1)S(1)} %collective-permute-done.13), channel_id=1, source_target_pairs={{0,1},{1,2},{2,3},{3,4},{4,5},{5,6},{6,7},{7,8},{8,9},{9,10},{10,1... | collective-permute-start | bytes 61448 | tf_op jit(solution)/shard_map/ppermute | solution.py:36
  121.8 9.1 %slice-start = ((s8[8847360]{0:T(1024)(128)(4,1)}), s8[4194304]{0:T(1024)(128)(4,1)S(1)}, s32[]{:S(2)}) async-start(s8[8847360]{0:T(1024)(128)(4,1)} %bitcast.12), calls=%async_computation.2 | async-start | bytes 8388608
  121.8 9.1 %slice-start.1 = ((s8[8847360]{0:T(1024)(128)(4,1)}), s8[4194304]{0:T(1024)(128)(4,1)S(1)}, s32[]{:S(2)}) async-start(s8[8847360]{0:T(1024)(128)(4,1)} %bitcast.12), calls=%async_computation.3 | async-start | bytes 8388608
  128.2 2.7 slice-start.2
  132.6 93.0 %copy-start.3 = (f32[5120]{0:T(1024)S(1)}, f32[5120]{0:T(1024)}, u32[]{:S(2)}) copy-start(f32[5120]{0:T(1024)} %param.13) | copy-start | bytes 61444
  135.1 196.5 %all-reduce.5.cloned.1.call-start = ((), (), s32[]{:S(2)}) async-start(), calls=%async_computation.1 | async-start | bytes 1310720 | tf_op jit(solution)/shard_map/psum | solution.py:59
  225.6 11.9 %slice-start.3 = ((s8[8847360]{0:T(1024)(128)(4,1)}), s8[4194304]{0:T(1024)(128)(4,1)S(1)}, s32[]{:S(2)}) async-start(s8[8847360]{0:T(1024)(128)(4,1)} %bitcast.14), calls=%async_computation.5 | async-start | bytes 8388608
  225.6 11.9 %slice-start.4 = ((s8[8847360]{0:T(1024)(128)(4,1)}), s8[458752]{0:T(1024)(128)(4,1)S(1)}, s32[]{:S(2)}) async-start(s8[8847360]{0:T(1024)(128)(4,1)} %bitcast.14), calls=%async_computation.6 | async-start | bytes 917504
  232.2 5.3 %slice-start.5 = ((s8[8847360]{0:T(1024)(128)(4,1)}), s8[4194304]{0:T(1024)(128)(4,1)S(1)}, s32[]{:S(2)}) async-start(s8[8847360]{0:T(1024)(128)(4,1)} %bitcast.14), calls=%async_computation.7 | async-start | bytes 8388608
  237.5 95.4 %copy-start.1 = (f32[32,5120]{1,0:T(8,128)S(1)}, f32[32,5120]{1,0:T(8,128)}, u32[]{:S(2)}) copy-start(f32[32,5120]{1,0:T(8,128)} %all-reduce.3.cloned.1.call-done) | copy-start | bytes 1966084
Sparse Core Ops, SparseCore 0:
  135.2 89.0 all-reduce.2
  240.1 91.4 all-reduce.4
